TPU v7x, 32 devices: a whole 2x2x4 slice. The times are simulated.
32 devices in a mesh: seq: 8 (over z, y), layer: 4 (over x, core).
Axes of the slice: x: 2, y: 2, z: 4, core: 2. Of those that a mesh axis runs over, the one named last changes fastest.
Arguments:
- gradients: bfloat16 [2048, 4096], P('seq', 'layer'), may hold values from -6 to 6
- projection: bfloat16 [4096, 8192], P('layer', 'seq'), may hold values from -0.09375 to 0.09375
- queries: bfloat16 [256, 8192], P(None, 'seq'), may hold values from -6 to 6
Outputs:
- scores: float32 [2048, 256], P(('seq', 'layer'))
All inputs are finite; a program needn't handle non-finite values.
Results may differ from a plain program's by a relative error of at most 0.0029.
Values may be sent and summed in bfloat16 or wider, within the bound.
A program may use at most 128 MiB of HBM per device.

v0:
```python
import math

import jax
import jax.numpy as jnp
from jax import lax
from jax.sharding import PartitionSpec as P

K = 8192


epsilon = 1e-06


def scaled(products, row_squares, query_squares):
    return (
        math.sqrt(K)
        * products
        * lax.rsqrt(row_squares + epsilon)[:, None]
        * lax.rsqrt(query_squares + epsilon)[None, :]
    )


def finish_columns(sketch, queries):
    sketch_wide = sketch.astype(jnp.float32)
    row_squares = lax.psum_scatter(
        jnp.sum(sketch_wide * sketch_wide, axis=1), "seq", scatter_dimension=0, tiled=True
    )
    query_wide = queries.astype(jnp.float32)
    query_squares = lax.psum(jnp.sum(query_wide * query_wide, axis=1), "seq")
    products = lax.psum_scatter(
        lax.dot_general(
            sketch, queries, (((1,), (1,)), ((), ())), preferred_element_type=jnp.float32
        ),
        "seq",
        scatter_dimension=0,
        tiled=True,
    )
    return scaled(products, row_squares, query_squares)


def shards(gradients, projection, queries):
    layers = lax.axis_size("layer")
    groups = lax.axis_size("seq")
    quarter = gradients.shape[0] // layers
    partial_value = jnp.dot(
        lax.all_gather(gradients, "seq", axis=0, tiled=True),
        projection,
        preferred_element_type=jnp.float32,
    )
    partial_value = partial_value.reshape(groups, layers, quarter, projection.shape[1])
    summed = lax.psum_scatter(partial_value, "layer", scatter_dimension=1, tiled=True)
    sketch = summed.reshape(groups * quarter, projection.shape[1]).astype(jnp.bfloat16)
    return finish_columns(sketch, queries)


def solution(mesh):
    placed = (P("seq", "layer"), P("layer", "seq"), P(None, "seq"))
    return jax.shard_map(
        shards, mesh=mesh, in_specs=placed, out_specs=P(("seq", "layer"), None), check_vma=False
    )
```

profile of v0, /device:TPU:0, one launch (start us, length us, event | category | flops | bytes accessed | tf_op | source)
XLA Modules:
  0.0 314.5 jit_solution(15314637607917910850)
XLA Ops:
  6.5 0.0 copy-start
  6.5 0.0 all-gather.2.cloned.1.call-start
  6.5 0.7 all-gather.2.cloned.1.call-update
  7.3 0.0 reduce-scatter.5.cloned.1.call-start
  7.3 1.2 dynamic-slice
  8.6 76.5 %all-gather.2.cloned.1.call-done = bf16[2048,1024]{1,0:T(8,128)(2,1)} async-done(((bf16[256,1024]{1,0:T(8,128)(2,1)}), bf16[2048,1024]{1,0:T(8,128)(2,1)}) %all-gather.2.cloned.1.call-update) | async-done | bytes 4194320 | tf_op jit(solution)/shard_map/all_gather | solution.py:46
  85.0 0.0 copy-done
  85.0 9.0 %fusion.2 = f32[2048,1024]{1,0:T(8,128)} fusion(bf16[2048,1024]{1,0:T(8,128)(2,1)} %all-gather.2.cloned.1.call-done, bf16[1024,1024]{1,0:T(8,128)(2,1)S(1)} %copy-done), kind=kOutput, calls=%fused_computation.8 | convolution fusion | flops 4294967296 | bytes 14680064 | tf_op jit(solution)/shard_map/dot_general | solution.py:45
  94.0 0.0 copy-start.1
  94.0 146.3 %all-reduce.4 = bf16[8,4,64,1024]{3,2,1,0:T(8,128)(2,1)} all-reduce(f32[8,4,64,1024]{3,2,1,0:T(8,128)} %bitcast.14), channel_id=2, replica_groups=mesh['seq'=8,'layer'=4] {'layer'}, use_global_device_ids=true, to_apply=%region_0.0.clone | all-reduce | flops 2097152 | bytes 12582912
  240.3 0.0 copy-start.2
  240.3 2.2 multiply_reduce_fusion
  242.5 0.0 copy-done.1
  242.5 1.3 fusion.3
  243.8 0.0 reduce-scatter.5.cloned.1.call-update
  243.8 0.0 copy-done.2
  243.8 0.6 dynamic-slice.2
  245.0 0.2 multiply_reduce_fusion.1
  245.2 0.1 reduce_sum.21
  245.3 20.2 %all-reduce.2 = (f32[256]{0:T(256)S(1)}, f32[512]{0:T(512)S(1)}) all-reduce(f32[256]{0:T(256)S(1)} %multiply_reduce_fusion.1, f32[512]{0:T(512)S(1)} %reduce_sum.21), channel_id=1, replica_groups=mesh['seq'=8,'layer'=4] {'seq'}, use_global_device_ids=true, to_apply=%region_5.0 | all-reduce | flops 768 | bytes 6144 | tf_op jit(solution)/shard_map/psum | solution.py:29
  265.5 0.1 fusion.1
  265.6 40.5 %reduce-scatter.5.cloned.1.call-done = f32[64,256]{1,0:T(8,128)} async-done(((f32[512,256]{1,0:T(8,128)}), f32[64,256]{1,0:T(8,128)}) %reduce-scatter.5.cloned.1.call-update) | async-done | bytes 65552 | tf_op jit(solution)/shard_map/reduce_scatter | solution.py:30
  306.1 1.5 multiply_multiply_fusion
  (1 shorter events, 0.0 us)
Async XLA Ops:
  6.5 78.5 %copy-start = (bf16[1024,1024]{1,0:T(8,128)(2,1)S(1)}, bf16[1024,1024]{1,0:T(8,128)(2,1)}, u32[]{:S(2)}) copy-start(bf16[1024,1024]{1,0:T(8,128)(2,1)} %param.4) | copy-start | bytes 6291460
  6.5 78.5 %all-gather.2.cloned.1.call-start = ((), (), s32[]{:S(2)}) async-start(), calls=%async_computation.1 | async-start | bytes 4718592 | tf_op jit(solution)/shard_map/all_gather | solution.py:46
  7.3 298.8 %reduce-scatter.5.cloned.1.call-start = ((), (), s32[]{:S(2)}) async-start(), calls=%async_computation.2 | async-start | bytes 589824 | tf_op jit(solution)/shard_map/reduce_scatter | solution.py:30
  94.0 148.5 %copy-start.1 = (bf16[256,1024]{1,0:T(8,128)(2,1)S(1)}, bf16[256,1024]{1,0:T(8,128)(2,1)}, u32[]{:S(2)}) copy-start(bf16[256,1024]{1,0:T(8,128)(2,1)} %param.5) | copy-start | bytes 1572868
  240.3 3.5 %copy-start.2 = (u32[32]{0:T(128)S(1)}, u32[32]{0:T(128)}, u32[]{:S(2)}) copy-start(u32[32]{0:T(128)} %constant.13) | copy-start | bytes 388
Sparse Core Ops, SparseCore 0:
  9.5 75.5 all-gather.1
  243.9 62.1 reduce-scatter.4
where the time goes:
time: 315 us; the launch traced here: 314 us
  blocking collectives  167 us (53%)
  waiting for transfers between devices  118 us (37%)
  between operations  14.1 us (4%)
  matrix products  10.3 us (3%)
  other arithmetic  3.98 us (1%)
    unnamed x1, blocking collectives  146 us
    all_gather x1, waiting for transfers between devices, shards(): lax.all_gather(gradients, 'seq', axis=0, tiled=True)  76.5 us
    reduce_scatter x1, waiting for transfers between devices, finish_columns(): lax.psum_scatter(lax.dot_general(sketch, queries, (((1,), (1,)), ((), ())...  40.5 us
    psum x1, blocking collectives, finish_columns(): query_squares = lax.psum(jnp.sum(query_wide * query_wide, axis=1), 'seq')  20.2 us
    dot_general x1, matrix products, shards(): jnp.dot(lax.all_gather(gradients, 'seq', axis=0, tiled=True), projection,...  8.98 us
  transfers between devices with their start and end apart: 2, of which 2 were waited for; matrix products, arithmetic and copies ran while one was open for 1% of the time, Pallas kernels for 0%

commit v1 on v0

v1 whole, which is shorter than its diff:
```python
import functools
import math

import jax
import jax.numpy as jnp
from jax import lax
from jax.experimental import pallas as pl
from jax.experimental.pallas import tpu as pltpu
from jax.sharding import PartitionSpec as P

epsilon = 1e-06
VMEM_BYTES = 60 * 2**20
MESH = pl.DeviceIdType.MESH


def scaled(width, products, row_squares, query_squares):
    return (
        math.sqrt(width)
        * products
        * lax.rsqrt(row_squares + epsilon)
        * lax.rsqrt(query_squares + epsilon)
    )


def kernel(
    groups, layers,
    g_ref, p_ref, q_ref, out_ref,
    gbuf, pother, qt, totals, xsend, xrecv, sbuf, rbuf,
    local_sem, core_sem, pair_sem, gsend, grecv, xsend_sem, xrecv_sem, rsend_sem, rrecv_sem,
):
    inner = 2
    outer = groups // inner
    banks = layers // 2
    rows = g_ref.shape[2]
    columns = p_ref.shape[1]
    asked = q_ref.shape[0]
    me, layer = lax.axis_index("seq"), lax.axis_index("layer")
    z, y = me // inner, me % inner
    x, c = layer // 2, layer % 2
    partner = x * 2 + 1 - c

    barrier = pltpu.get_barrier_semaphore()
    for step in range(1, groups):
        pl.semaphore_signal(
            barrier, inc=1, device_id=((me + step) % groups, layer), device_id_type=MESH
        )
    for step in range(1, layers):
        pl.semaphore_signal(
            barrier, inc=1, device_id=(me, (layer + step) % layers), device_id_type=MESH
        )
    pl.semaphore_wait(barrier, groups + layers - 2)

    def remote(src, dst, send, recv, group, layer_to):
        return pltpu.make_async_remote_copy(
            src_ref=src, dst_ref=dst, send_sem=send, recv_sem=recv,
            device_id=(group, layer_to), device_id_type=MESH,
        )

    own = pltpu.make_async_copy(g_ref.at[:, c], gbuf.at[me, 0], local_sem)
    own.start()
    swap_g = remote(
        g_ref.at[:, 1 - c], gbuf.at[me, 1], core_sem, grecv.at[me, 1], me, partner
    )
    swap_g.start()
    swap_p = remote(p_ref, pother, pair_sem.at[0], pair_sem.at[1], me, partner)
    swap_p.start()
    own.wait()

    reach = jnp.minimum(z, outer - 1 - z)

    def source(t):
        half = (t + 1) // 2
        near = z + half * (2 * (t % 2) - 1)
        far = jnp.where(z <= outer - 1 - z, t, outer - 1 - t)
        return jnp.where(t <= 2 * reach, near, far)

    def chunk(block, part, link, group):
        return remote(
            gbuf.at[block, part], gbuf.at[block, part],
            gsend.at[block, part, link], grecv.at[block, part], group, layer,
        )

    def links(src, act):
        block = src * inner + y

        def send(part):
            act(chunk(block, part, 0, z * inner + 1 - y))

            @pl.when((src <= z) & (z < outer - 1))
            def _():
                act(chunk(block, part, 1, (z + 1) * inner + y))

            @pl.when((src >= z) & (z > 0))
            def _():
                act(chunk(block, part, 2, (z - 1) * inner + y))

        return send

    tile = min(columns, 256)

    def multiply(block):
        @pl.loop(0, columns // tile)
        def _(k):
            cols = pl.ds(pl.multiple_of(k * tile, tile), tile)
            first = gbuf[block, 0].reshape(banks * rows, -1)
            second = gbuf[block, 1].reshape(banks * rows, -1)
            total = jnp.dot(first, p_ref[:, cols], preferred_element_type=jnp.float32)
            total += jnp.dot(second, pother[:, cols], preferred_element_type=jnp.float32)
            total = total.reshape(banks, rows, tile)
            totals[block, :, :, cols] = total
            xsend[block, :, :, cols] = total.astype(jnp.bfloat16)

        for step in range(1, banks):
            exchange(block, step).start()

    def exchange(block, step):
        to = (x + step) % banks
        return remote(
            xsend.at[block, to], xrecv.at[block, step - 1],
            xsend_sem.at[block, step - 1], xrecv_sem.at[block, step - 1],
            me, to * 2 + c,
        )

    def deliver(block):
        return remote(
            sbuf.at[block], rbuf.at[me], rsend_sem.at[block], rrecv_sem.at[me], block, layer
        )

    def finish(block):
        sketch = totals[block, x]
        for step in range(1, banks):
            exchange(block, step).wait_recv()
            sketch += xrecv[block, step - 1].astype(jnp.float32)
        high = sketch.astype(jnp.bfloat16)
        low = (sketch - high.astype(jnp.float32)).astype(jnp.bfloat16)
        both = jnp.dot(
            jnp.concatenate([high, low], axis=0), qt[...], preferred_element_type=jnp.float32
        )
        squares = jnp.sum(sketch * sketch, axis=1, keepdims=True)
        sbuf[block, :rows] = both[:rows] + both[rows:]
        sbuf[block, rows : rows + 8, :rows] = jnp.broadcast_to(squares, (rows, 128)).T[:8]

        @pl.when(block != me)
        def _():
            deliver(block).start()

    wide = q_ref[...].T
    qt[...] = wide
    wide = wide.astype(jnp.float32)
    query_part = jnp.sum(wide * wide, axis=0, keepdims=True)

    @pl.loop(0, groups)
    def _(block):
        sbuf[block, rows + 8 :] = jnp.broadcast_to(query_part, (8, asked))

    @pl.loop(0, outer + 2)
    def _(t):
        @pl.when(t < outer)
        def _():
            src = source(t)
            block = src * inner + y
            for part in range(2):
                if part == 0:
                    @pl.when(t > 0)
                    def _():
                        chunk(block, 0, 0, me).wait_recv()
                else:
                    chunk(block, 1, 0, me).wait_recv()
                links(src, lambda copy: copy.start())(part)

            @pl.when(t == 0)
            def _():
                swap_p.wait_recv()

            multiply(block)

        @pl.when((t >= 1) & (t <= outer))
        def _():
            finish(source(t - 1) * inner + y)
            block = source(t - 1) * inner + 1 - y
            for part in range(2):
                chunk(block, part, 0, me).wait_recv()
            multiply(block)

        @pl.when(t >= 2)
        def _():
            finish(source(t - 2) * inner + 1 - y)

    products = sbuf[me]

    def collect(step, total):
        block = (me + step) % groups
        remote(
            sbuf.at[block], rbuf.at[block], rsend_sem.at[block], rrecv_sem.at[block],
            block, layer,
        ).wait_recv()
        return total + rbuf[block]

    products = lax.fori_loop(1, groups, collect, products)
    squares = jnp.broadcast_to(products[rows : rows + 1, :rows], (128, rows)).T[:, :1]
    out_ref[...] = scaled(
        columns * groups, products[:rows], squares, products[rows + 8 : rows + 9]
    )

    swap_g.wait_send()
    swap_p.wait_send()

    @pl.loop(0, outer)
    def _(t):
        src = source(t)
        for part in range(2):
            links(src, lambda copy: copy.wait_send())(part)

    @pl.loop(0, groups)
    def _(block):
        for step in range(1, banks):
            exchange(block, step).wait_send()

        @pl.when(block != me)
        def _():
            deliver(block).wait_send()


def scratch(groups, layers, gradients, projection, queries):
    banks, rows = layers // 2, gradients[0] // layers
    features, columns = projection
    asked = queries[0]
    message = (groups, rows + 16, asked)
    return [
        ((groups, 2, banks, rows, features), jnp.bfloat16),
        ((features, columns), jnp.bfloat16),
        ((columns, asked), jnp.bfloat16),
        ((groups, banks, rows, columns), jnp.float32),
        ((groups, banks, rows, columns), jnp.bfloat16),
        ((groups, max(banks - 1, 1), rows, columns), jnp.bfloat16),
        (message, jnp.float32),
        (message, jnp.float32),
    ]


def fused(groups, layers, gradients, projection, queries):
    banks = layers // 2
    rows = gradients.shape[0] // layers
    buffers = scratch(groups, layers, gradients.shape, projection.shape, queries.shape)
    dma = pltpu.SemaphoreType.DMA
    spread = max(banks - 1, 1)
    return pl.pallas_call(
        functools.partial(kernel, groups, layers),
        out_shape=jax.ShapeDtypeStruct((rows, queries.shape[0]), jnp.float32),
        in_specs=[pl.BlockSpec(memory_space=pltpu.VMEM)] * 3,
        out_specs=pl.BlockSpec(memory_space=pltpu.VMEM),
        scratch_shapes=[pltpu.VMEM(shape, kind) for shape, kind in buffers]
        + [
            dma, dma, dma((2,)), dma((groups, 2, 3)), dma((groups, 2)),
            dma((groups, spread)), dma((groups, spread)), dma((groups,)), dma((groups,)),
        ],
        compiler_params=pltpu.CompilerParams(
            collective_id=0, has_side_effects=True, vmem_limit_bytes=VMEM_BYTES
        ),
    )(gradients.reshape(banks, 2, rows, gradients.shape[1]), projection, queries)


def plain(groups, layers, gradients, projection, queries):
    quarter = gradients.shape[0] // layers
    partial_value = jnp.dot(
        lax.all_gather(gradients, "seq", axis=0, tiled=True),
        projection,
        preferred_element_type=jnp.float32,
    )
    partial_value = partial_value.reshape(groups, layers, quarter, projection.shape[1])
    summed = lax.psum_scatter(partial_value, "layer", scatter_dimension=1, tiled=True)
    sketch = summed.reshape(groups * quarter, projection.shape[1]).astype(jnp.bfloat16)
    sketch_wide = sketch.astype(jnp.float32)
    row_squares = lax.psum_scatter(
        jnp.sum(sketch_wide * sketch_wide, axis=1), "seq", scatter_dimension=0, tiled=True
    )
    query_wide = queries.astype(jnp.float32)
    query_squares = lax.psum(jnp.sum(query_wide * query_wide, axis=1), "seq")
    products = lax.psum_scatter(
        lax.dot_general(
            sketch, queries, (((1,), (1,)), ((), ())), preferred_element_type=jnp.float32
        ),
        "seq",
        scatter_dimension=0,
        tiled=True,
    )
    width = projection.shape[1] * groups
    return scaled(width, products, row_squares[:, None], query_squares[None, :])


def shards(gradients, projection, queries):
    layers = lax.axis_size("layer")
    groups = lax.axis_size("seq")
    rows = gradients.shape[0] // layers
    needed = sum(
        math.prod(shape) * jnp.dtype(kind).itemsize
        for shape, kind in scratch(
            groups, layers, gradients.shape, projection.shape, queries.shape
        )
    ) + 2 * (gradients.size + projection.size + queries.size)
    fits = (
        groups % 2 == 0
        and layers % 2 == 0
        and rows % 16 == 0
        and rows <= min(128, queries.shape[0])
        and needed < VMEM_BYTES - 8 * 2**20
    )
    path = fused if fits else plain
    return path(groups, layers, gradients, projection, queries)


def solution(mesh):
    placed = (P("seq", "layer"), P("layer", "seq"), P(None, "seq"))
    return jax.shard_map(
        shards, mesh=mesh, in_specs=placed, out_specs=P(("seq", "layer"), None), check_vma=False
    )
```

time: 315 us -> 73.4 us (0.23)
  blocking collectives: 167 us -> 0 us
  waiting for transfers between devices: 118 us -> 0 us
  Pallas kernels: 0 us -> 71.8 us
  between operations: 14.1 us -> 0.01 us
  matrix products: 10.3 us -> 0 us
  other arithmetic: 3.98 us -> 0 us
    unnamed x1 -> x0, blocking collectives: 146 us -> none
    all_gather x1 -> x0, waiting for transfers between devices: 76.5 us -> none  [shards(): lax.all_gather(gradients, 'seq', axis=0, tiled=True)]
    pallas_call x0 -> x1, Pallas kernels: none -> 71.8 us  [fused(): pl.pallas_call(functools.partial(kernel, groups, layers), out_shape=jax.S...]
    reduce_scatter x1 -> x0, waiting for transfers between devices: 40.5 us -> none  [finish_columns(): lax.psum_scatter(lax.dot_general(sketch, queries, (((1,), (1,)), ((), ())...]
    psum x1 -> x0, blocking collectives: 20.2 us -> none  [finish_columns(): query_squares = lax.psum(jnp.sum(query_wide * query_wide, axis=1), 'seq')]
    dot_general x2 -> x0, matrix products: 10.3 us -> none  [the longest x1 8.98 us: shards(): jnp.dot(lax.all_gather(gradients, 'seq', axis=0, tiled=True), projection,...]
  transfers between devices with their start and end apart: 2 -> 0, of which waited for: 2 -> 0; matrix products, arithmetic and copies ran while one was open for 1% -> 0% of each run, Pallas kernels for 0% -> 0%
where the time goes in v1:
time: 73.4 us; the launch traced here: 73.3 us
  Pallas kernels  71.8 us (98%)
  local copies, waits for them, and re-layouts  1.47 us (2%)
    pallas_call x1, Pallas kernels, fused(): pl.pallas_call(functools.partial(kernel, groups, layers), out_shape=jax.S...  71.8 us
    unnamed x1, local copies, waits for them, and re-layouts  1.47 us

profile of v1, /device:TPU:0, one launch (start us, length us, event | category | flops | bytes accessed | tf_op | source)
XLA Modules:
  0.0 73.3 jit_solution(4820843911069629377)
XLA Ops:
  0.0 71.8 %shard_map.37 = f32[64,256]{1,0:T(8,128)} custom-call(bf16[2,2,64,1024]{3,2,1,0:T(8,128)(2,1)} %bitcast.1, bf16[1024,1024]{1,0:T(8,128)(2,1)} %p_ref.1, bf16[256,1024]{1,0:T(8,128)(2,1)} %q_ref.1), custom_call_target="tpu_custom_call" | custom-call | tf_op jit(solution)/shard_map/pallas_call | solution.py:247
  71.8 1.5 %copy.5 = f32[64,256]{1,0:T(8,128)} copy(f32[64,256]{1,0:T(8,128)} %shard_map.37) | data formatting | bytes 131072

commit v2 on v1

--- a/solution.py
+++ b/solution.py
@@ -24,14 +24,14 @@
 
 def kernel(
     groups, layers,
-    g_ref, p_ref, q_ref, out_ref,
-    gbuf, pother, qt, totals, xsend, xrecv, sbuf, rbuf,
+    g_hbm, p_hbm, q_hbm, out_ref,
+    p_ref, q_ref, gbuf, pother, qt, totals, xsend, xrecv, sbuf, rbuf,
     local_sem, core_sem, pair_sem, gsend, grecv, xsend_sem, xrecv_sem, rsend_sem, rrecv_sem,
 ):
     inner = 2
     outer = groups // inner
     banks = layers // 2
-    rows = g_ref.shape[2]
+    rows = g_hbm.shape[2]
     columns = p_ref.shape[1]
     asked = q_ref.shape[0]
     me, layer = lax.axis_index("seq"), lax.axis_index("layer")
@@ -39,16 +39,35 @@
     x, c = layer // 2, layer % 2
     partner = x * 2 + 1 - c
 
+    own = pltpu.make_async_copy(g_hbm.at[:, c], gbuf.at[me, 0], local_sem.at[0])
+    own.start()
+    load_p = pltpu.make_async_copy(p_hbm, p_ref, local_sem.at[1])
+    load_p.start()
+    load_q = pltpu.make_async_copy(q_hbm, q_ref, local_sem.at[2])
+    load_q.start()
+
     barrier = pltpu.get_barrier_semaphore()
-    for step in range(1, groups):
+
+    def greet(group, layer_to):
         pl.semaphore_signal(
-            barrier, inc=1, device_id=((me + step) % groups, layer), device_id_type=MESH
-        )
-    for step in range(1, layers):
-        pl.semaphore_signal(
-            barrier, inc=1, device_id=(me, (layer + step) % layers), device_id_type=MESH
-        )
-    pl.semaphore_wait(barrier, groups + layers - 2)
+            barrier, inc=1, device_id=(group, layer_to), device_id_type=MESH
+        )
+
+    greet(me, partner)
+    greet(z * inner + 1 - y, layer)
+    for step in range(1, banks):
+        greet(me, (x + step) % banks * 2 + c)
+
+    @pl.when(z > 0)
+    def _():
+        greet(me - inner, layer)
+
+    @pl.when(z < outer - 1)
+    def _():
+        greet(me + inner, layer)
+
+    ends = jnp.minimum(z, 1) + jnp.minimum(outer - 1 - z, 1)
+    pl.semaphore_wait(barrier, banks + 1 + ends)
 
     def remote(src, dst, send, recv, group, layer_to):
         return pltpu.make_async_remote_copy(
@@ -56,15 +75,10 @@
             device_id=(group, layer_to), device_id_type=MESH,
         )
 
-    own = pltpu.make_async_copy(g_ref.at[:, c], gbuf.at[me, 0], local_sem)
-    own.start()
     swap_g = remote(
-        g_ref.at[:, 1 - c], gbuf.at[me, 1], core_sem, grecv.at[me, 1], me, partner
+        g_hbm.at[:, 1 - c], gbuf.at[me, 1], core_sem, grecv.at[me, 1], me, partner
     )
     swap_g.start()
-    swap_p = remote(p_ref, pother, pair_sem.at[0], pair_sem.at[1], me, partner)
-    swap_p.start()
-    own.wait()
 
     reach = jnp.minimum(z, outer - 1 - z)
 
@@ -80,21 +94,39 @@
             gsend.at[block, part, link], grecv.at[block, part], group, layer,
         )
 
-    def links(src, act):
+    up, down = z < outer - 1, z > 0
+
+    def relay(src, part, act):
         block = src * inner + y
 
-        def send(part):
+        @pl.when((part == 0) | (src == z) | ((src > 0) & (src < outer - 1)))
+        def _():
             act(chunk(block, part, 0, z * inner + 1 - y))
 
-            @pl.when((src <= z) & (z < outer - 1))
-            def _():
-                act(chunk(block, part, 1, (z + 1) * inner + y))
-
-            @pl.when((src >= z) & (z > 0))
-            def _():
-                act(chunk(block, part, 2, (z - 1) * inner + y))
-
-        return send
+        @pl.when((src <= z) & up)
+        def _():
+            act(chunk(block, part, 1, me + inner))
+
+        @pl.when((src >= z) & down)
+        def _():
+            act(chunk(block, part, 2, me - inner))
+
+    def relay_other(src, act):
+        block = src * inner + 1 - y
+
+        @pl.when((src == 0) & up)
+        def _():
+            act(chunk(block, 1, 1, me + inner))
+
+        @pl.when((src == outer - 1) & down)
+        def _():
+            act(chunk(block, 1, 2, me - inner))
+
+    def start(copy):
+        copy.start()
+
+    def drain(copy):
+        copy.wait_send()
 
     tile = min(columns, 256)
 
@@ -138,11 +170,19 @@
         )
         squares = jnp.sum(sketch * sketch, axis=1, keepdims=True)
         sbuf[block, :rows] = both[:rows] + both[rows:]
-        sbuf[block, rows : rows + 8, :rows] = jnp.broadcast_to(squares, (rows, 128)).T[:8]
+        sbuf[block, rows : rows + 1, :rows] = jnp.broadcast_to(squares, (rows, 128)).T[:1]
 
         @pl.when(block != me)
         def _():
             deliver(block).start()
+
+    own.wait()
+    relay(z, 0, start)
+    swap_p = remote(p_hbm, pother, pair_sem.at[0], pair_sem.at[1], me, partner)
+    swap_p.start()
+    chunk(me, 1, 0, me).wait_recv()
+    relay(z, 1, start)
+    load_q.wait()
 
     wide = q_ref[...].T
     qt[...] = wide
@@ -151,7 +191,10 @@
 
     @pl.loop(0, groups)
     def _(block):
-        sbuf[block, rows + 8 :] = jnp.broadcast_to(query_part, (8, asked))
+        sbuf[block, rows + 1 : rows + 2] = query_part
+
+    load_p.wait()
+    swap_p.wait_recv()
 
     @pl.loop(0, outer + 2)
     def _(t):
@@ -159,18 +202,11 @@
         def _():
             src = source(t)
             block = src * inner + y
-            for part in range(2):
-                if part == 0:
-                    @pl.when(t > 0)
-                    def _():
-                        chunk(block, 0, 0, me).wait_recv()
-                else:
-                    chunk(block, 1, 0, me).wait_recv()
-                links(src, lambda copy: copy.start())(part)
-
-            @pl.when(t == 0)
+            @pl.when(t > 0)
             def _():
-                swap_p.wait_recv()
+                for part in range(2):
+                    chunk(block, part, 0, me).wait_recv()
+                    relay(src, part, start)
 
             multiply(block)
 
@@ -180,6 +216,7 @@
             block = source(t - 1) * inner + 1 - y
             for part in range(2):
                 chunk(block, part, 0, me).wait_recv()
+            relay_other(source(t - 1), start)
             multiply(block)
 
         @pl.when(t >= 2)
@@ -199,7 +236,7 @@
     products = lax.fori_loop(1, groups, collect, products)
     squares = jnp.broadcast_to(products[rows : rows + 1, :rows], (128, rows)).T[:, :1]
     out_ref[...] = scaled(
-        columns * groups, products[:rows], squares, products[rows + 8 : rows + 9]
+        columns * groups, products[:rows], squares, products[rows + 1 : rows + 2]
     )
 
     swap_g.wait_send()
@@ -209,7 +246,8 @@
     def _(t):
         src = source(t)
         for part in range(2):
-            links(src, lambda copy: copy.wait_send())(part)
+            relay(src, part, drain)
+        relay_other(src, drain)
 
     @pl.loop(0, groups)
     def _(block):
@@ -225,8 +263,10 @@
     banks, rows = layers // 2, gradients[0] // layers
     features, columns = projection
     asked = queries[0]
-    message = (groups, rows + 16, asked)
+    message = (groups, rows + 8, asked)
     return [
+        ((features, columns), jnp.bfloat16),
+        ((asked, columns), jnp.bfloat16),
         ((groups, 2, banks, rows, features), jnp.bfloat16),
         ((features, columns), jnp.bfloat16),
         ((columns, asked), jnp.bfloat16),
@@ -247,11 +287,11 @@
     return pl.pallas_call(
         functools.partial(kernel, groups, layers),
         out_shape=jax.ShapeDtypeStruct((rows, queries.shape[0]), jnp.float32),
-        in_specs=[pl.BlockSpec(memory_space=pltpu.VMEM)] * 3,
+        in_specs=[pl.BlockSpec(memory_space=pl.ANY)] * 3,
         out_specs=pl.BlockSpec(memory_space=pltpu.VMEM),
         scratch_shapes=[pltpu.VMEM(shape, kind) for shape, kind in buffers]
         + [
-            dma, dma, dma((2,)), dma((groups, 2, 3)), dma((groups, 2)),
+            dma((3,)), dma, dma((2,)), dma((groups, 2, 3)), dma((groups, 2)),
             dma((groups, spread)), dma((groups, spread)), dma((groups,)), dma((groups,)),
         ],
         compiler_params=pltpu.CompilerParams(
@@ -297,7 +337,7 @@
         for shape, kind in scratch(
             groups, layers, gradients.shape, projection.shape, queries.shape
         )
-    ) + 2 * (gradients.size + projection.size + queries.size)
+    )
     fits = (
         groups % 2 == 0
         and layers % 2 == 0

time: 73.4 us -> 72.7 us (level)
  no operation moved by 1% of the time
where the time goes in v2:
time: 72.7 us; the launch traced here: 72.6 us
  Pallas kernels  71.1 us (98%)
  local copies, waits for them, and re-layouts  1.47 us (2%)
    pallas_call x1, Pallas kernels, fused(): pl.pallas_call(functools.partial(kernel, groups, layers), out_shape=jax.S...  71.1 us
    unnamed x1, local copies, waits for them, and re-layouts  1.47 us

profile of v2, /device:TPU:0, one launch (start us, length us, event | category | flops | bytes accessed | tf_op | source)
XLA Modules:
  0.0 72.6 jit_solution(1076562216996998732)
XLA Ops:
  0.0 71.1 %shard_map.37 = f32[64,256]{1,0:T(8,128)} custom-call(bf16[2,2,64,1024]{3,2,1,0:T(8,128)(2,1)} %bitcast.1, bf16[1024,1024]{1,0:T(8,128)(2,1)} %p_hbm.1, bf16[256,1024]{1,0:T(8,128)(2,1)} %q_hbm.1), custom_call_target="tpu_custom_call" | custom-call | tf_op jit(solution)/shard_map/pallas_call | solution.py:287
  71.1 1.5 %copy.5 = f32[64,256]{1,0:T(8,128)} copy(f32[64,256]{1,0:T(8,128)} %shard_map.37) | data formatting | bytes 131072

commit v3 on v2

--- a/solution.py
+++ b/solution.py
@@ -25,7 +25,7 @@
 def kernel(
     groups, layers,
     g_hbm, p_hbm, q_hbm, out_ref,
-    p_ref, q_ref, gbuf, pother, qt, totals, xsend, xrecv, sbuf, rbuf,
+    p_ref, q_ref, gbuf, pother, qt, totals, xsend, xrecv, sbuf, rbuf, mine,
     local_sem, core_sem, pair_sem, gsend, grecv, xsend_sem, xrecv_sem, rsend_sem, rrecv_sem,
 ):
     inner = 2
@@ -84,7 +84,8 @@
 
     def source(t):
         half = (t + 1) // 2
-        near = z + half * (2 * (t % 2) - 1)
+        side = jnp.where(2 * z < outer, 1, -1)
+        near = z + side * half * (2 * (t % 2) - 1)
         far = jnp.where(z <= outer - 1 - z, t, outer - 1 - t)
         return jnp.where(t <= 2 * reach, near, far)
 
@@ -169,12 +170,28 @@
             jnp.concatenate([high, low], axis=0), qt[...], preferred_element_type=jnp.float32
         )
         squares = jnp.sum(sketch * sketch, axis=1, keepdims=True)
-        sbuf[block, :rows] = both[:rows] + both[rows:]
-        sbuf[block, rows : rows + 1, :rows] = jnp.broadcast_to(squares, (rows, 128)).T[:1]
+        products = both[:rows] + both[rows:]
+        squares = jnp.broadcast_to(squares, (rows, 128)).T[:1]
+
+        @pl.when(block == me)
+        def _():
+            mine[:rows] = products
+            mine[rows : rows + 1, :rows] = squares
 
         @pl.when(block != me)
         def _():
+            sbuf[block, :rows] = products.astype(jnp.bfloat16)
+            pieces = jnp.concatenate(split(squares), axis=0)
+            sbuf[block, rows : rows + 8, :rows] = pieces
             deliver(block).start()
+
+    def split(exact):
+        pieces = []
+        for _ in range(3):
+            piece = exact.astype(jnp.bfloat16)
+            pieces.append(piece)
+            exact -= piece.astype(jnp.float32)
+        return pieces + [jnp.zeros((5, exact.shape[1]), jnp.bfloat16)]
 
     own.wait()
     relay(z, 0, start)
@@ -189,14 +206,20 @@
     wide = wide.astype(jnp.float32)
     query_part = jnp.sum(wide * wide, axis=0, keepdims=True)
 
+    mine[rows:] = jnp.zeros((16, asked), jnp.float32)
+    mine[rows + 8 : rows + 9] = query_part
+    query_pieces = jnp.concatenate(split(query_part), axis=0)
+
     @pl.loop(0, groups)
     def _(block):
-        sbuf[block, rows + 1 : rows + 2] = query_part
+        sbuf[block, rows + 8 :] = query_pieces
 
     load_p.wait()
     swap_p.wait_recv()
 
-    @pl.loop(0, outer + 2)
+    lag = 1 + jnp.minimum(reach, 1)
+
+    @pl.loop(0, outer + 3)
     def _(t):
         @pl.when(t < outer)
         def _():
@@ -213,17 +236,21 @@
         @pl.when((t >= 1) & (t <= outer))
         def _():
             finish(source(t - 1) * inner + y)
-            block = source(t - 1) * inner + 1 - y
+
+        @pl.when((t >= lag) & (t < lag + outer))
+        def _():
+            src = source(t - lag)
+            block = src * inner + 1 - y
             for part in range(2):
                 chunk(block, part, 0, me).wait_recv()
-            relay_other(source(t - 1), start)
+            relay_other(src, start)
             multiply(block)
 
-        @pl.when(t >= 2)
-        def _():
-            finish(source(t - 2) * inner + 1 - y)
-
-    products = sbuf[me]
+        @pl.when((t > lag) & (t <= lag + outer))
+        def _():
+            finish(source(t - lag - 1) * inner + 1 - y)
+
+    products = mine[...]
 
     def collect(step, total):
         block = (me + step) % groups
@@ -231,12 +258,13 @@
             sbuf.at[block], rbuf.at[block], rsend_sem.at[block], rrecv_sem.at[block],
             block, layer,
         ).wait_recv()
-        return total + rbuf[block]
+        return total + rbuf[block].astype(jnp.float32)
 
     products = lax.fori_loop(1, groups, collect, products)
-    squares = jnp.broadcast_to(products[rows : rows + 1, :rows], (128, rows)).T[:, :1]
+    squares = products[rows : rows + 8, :rows].sum(axis=0, keepdims=True)
+    squares = jnp.broadcast_to(squares, (128, rows)).T[:, :1]
     out_ref[...] = scaled(
-        columns * groups, products[:rows], squares, products[rows + 1 : rows + 2]
+        columns * groups, products[:rows], squares, products[rows + 8 :].sum(axis=0, keepdims=True)
     )
 
     swap_g.wait_send()
@@ -263,7 +291,7 @@
     banks, rows = layers // 2, gradients[0] // layers
     features, columns = projection
     asked = queries[0]
-    message = (groups, rows + 8, asked)
+    message = (groups, rows + 16, asked)
     return [
         ((features, columns), jnp.bfloat16),
         ((asked, columns), jnp.bfloat16),
@@ -273,8 +301,9 @@
         ((groups, banks, rows, columns), jnp.float32),
         ((groups, banks, rows, columns), jnp.bfloat16),
         ((groups, max(banks - 1, 1), rows, columns), jnp.bfloat16),
-        (message, jnp.float32),
-        (message, jnp.float32),
+        (message, jnp.bfloat16),
+        (message, jnp.bfloat16),
+        (message[1:], jnp.float32),
     ]
 
 

time: 72.7 us -> 62.4 us (0.86)
  Pallas kernels: 71.1 us -> 60.8 us
    pallas_call x1, Pallas kernels: 71.1 us -> 60.8 us  [fused(): pl.pallas_call(functools.partial(kernel, groups, layers), out_shape=jax.S...]
where the time goes in v3:
time: 62.4 us; the launch traced here: 62.3 us
  Pallas kernels  60.8 us (97%)
  local copies, waits for them, and re-layouts  1.47 us (2%)
    pallas_call x1, Pallas kernels, fused(): pl.pallas_call(functools.partial(kernel, groups, layers), out_shape=jax.S...  60.8 us
    unnamed x1, local copies, waits for them, and re-layouts  1.47 us

profile of v3, /device:TPU:0, one launch (start us, length us, event | category | flops | bytes accessed | tf_op | source)
XLA Modules:
  0.0 62.3 jit_solution(5922332545089937415)
XLA Ops:
  0.0 60.8 %shard_map.37 = f32[64,256]{1,0:T(8,128)} custom-call(bf16[2,2,64,1024]{3,2,1,0:T(8,128)(2,1)} %bitcast.1, bf16[1024,1024]{1,0:T(8,128)(2,1)} %p_hbm.1, bf16[256,1024]{1,0:T(8,128)(2,1)} %q_hbm.1), custom_call_target="tpu_custom_call" | custom-call | tf_op jit(solution)/shard_map/pallas_call | solution.py:316
  60.8 1.5 %copy.5 = f32[64,256]{1,0:T(8,128)} copy(f32[64,256]{1,0:T(8,128)} %shard_map.37) | data formatting | bytes 131072

commit v4 on v3

--- a/solution.py
+++ b/solution.py
@@ -10,6 +10,7 @@
 
 epsilon = 1e-06
 VMEM_BYTES = 60 * 2**20
+TILE = 512
 MESH = pl.DeviceIdType.MESH
 
 
@@ -129,28 +130,38 @@
     def drain(copy):
         copy.wait_send()
 
-    tile = min(columns, 256)
-
-    def multiply(block):
+    tile = min(columns, TILE)
+
+    def part_product(block, part, weights, cols):
+        left = gbuf[block, part].reshape(banks * rows, -1)
+        product = jnp.dot(left, weights[:, cols], preferred_element_type=jnp.float32)
+        return product.reshape(banks, rows, tile)
+
+    def columns_of(k):
+        return pl.ds(pl.multiple_of(k * tile, tile), tile)
+
+    def begin(block):
         @pl.loop(0, columns // tile)
         def _(k):
-            cols = pl.ds(pl.multiple_of(k * tile, tile), tile)
-            first = gbuf[block, 0].reshape(banks * rows, -1)
-            second = gbuf[block, 1].reshape(banks * rows, -1)
-            total = jnp.dot(first, p_ref[:, cols], preferred_element_type=jnp.float32)
-            total += jnp.dot(second, pother[:, cols], preferred_element_type=jnp.float32)
-            total = total.reshape(banks, rows, tile)
+            cols = columns_of(k)
+            totals[block, :, :, cols] = part_product(block, 0, p_ref, cols)
+
+    def complete(block):
+        @pl.loop(0, columns // tile)
+        def _(k):
+            cols = columns_of(k)
+            total = totals[block, :, :, cols] + part_product(block, 1, pother, cols)
             totals[block, :, :, cols] = total
             xsend[block, :, :, cols] = total.astype(jnp.bfloat16)
-
-        for step in range(1, banks):
-            exchange(block, step).start()
-
-    def exchange(block, step):
+            for step in range(1, banks):
+                exchange(block, step, k).start()
+
+    def exchange(block, step, k):
         to = (x + step) % banks
+        cols = columns_of(k)
         return remote(
-            xsend.at[block, to], xrecv.at[block, step - 1],
-            xsend_sem.at[block, step - 1], xrecv_sem.at[block, step - 1],
+            xsend.at[block, to, :, cols], xrecv.at[block, step - 1, :, cols],
+            xsend_sem.at[block, step - 1, k], xrecv_sem.at[block, step - 1, k],
             me, to * 2 + c,
         )
 
@@ -162,7 +173,8 @@
     def finish(block):
         sketch = totals[block, x]
         for step in range(1, banks):
-            exchange(block, step).wait_recv()
+            for k in range(columns // tile):
+                exchange(block, step, k).wait_recv()
             sketch += xrecv[block, step - 1].astype(jnp.float32)
         high = sketch.astype(jnp.bfloat16)
         low = (sketch - high.astype(jnp.float32)).astype(jnp.bfloat16)
@@ -231,7 +243,8 @@
                     chunk(block, part, 0, me).wait_recv()
                     relay(src, part, start)
 
-            multiply(block)
+            begin(block)
+            complete(block)
 
         @pl.when((t >= 1) & (t <= outer))
         def _():
@@ -241,10 +254,11 @@
         def _():
             src = source(t - lag)
             block = src * inner + 1 - y
-            for part in range(2):
-                chunk(block, part, 0, me).wait_recv()
+            chunk(block, 0, 0, me).wait_recv()
+            begin(block)
+            chunk(block, 1, 0, me).wait_recv()
             relay_other(src, start)
-            multiply(block)
+            complete(block)
 
         @pl.when((t > lag) & (t <= lag + outer))
         def _():
@@ -280,7 +294,8 @@
     @pl.loop(0, groups)
     def _(block):
         for step in range(1, banks):
-            exchange(block, step).wait_send()
+            for k in range(columns // tile):
+                exchange(block, step, k).wait_send()
 
         @pl.when(block != me)
         def _():
@@ -313,6 +328,8 @@
     buffers = scratch(groups, layers, gradients.shape, projection.shape, queries.shape)
     dma = pltpu.SemaphoreType.DMA
     spread = max(banks - 1, 1)
+    columns = projection.shape[1]
+    tiles = columns // min(columns, TILE)
     return pl.pallas_call(
         functools.partial(kernel, groups, layers),
         out_shape=jax.ShapeDtypeStruct((rows, queries.shape[0]), jnp.float32),
@@ -321,7 +338,7 @@
         scratch_shapes=[pltpu.VMEM(shape, kind) for shape, kind in buffers]
         + [
             dma((3,)), dma, dma((2,)), dma((groups, 2, 3)), dma((groups, 2)),
-            dma((groups, spread)), dma((groups, spread)), dma((groups,)), dma((groups,)),
+            dma((groups, spread, tiles)), dma((groups, spread, tiles)), dma((groups,)), dma((groups,)),
         ],
         compiler_params=pltpu.CompilerParams(
             collective_id=0, has_side_effects=True, vmem_limit_bytes=VMEM_BYTES
@@ -371,6 +388,8 @@
         groups % 2 == 0
         and layers % 2 == 0
         and rows % 16 == 0
+        and projection.shape[1] % min(projection.shape[1], TILE) == 0
+        and min(projection.shape[1], TILE) % 128 == 0
         and rows <= min(128, queries.shape[0])
         and needed < VMEM_BYTES - 8 * 2**20
     )

time: 62.4 us -> 61.6 us (0.987)
  Pallas kernels: 60.8 us -> 59.9 us
    pallas_call x1, Pallas kernels: 60.8 us -> 59.9 us  [fused(): pl.pallas_call(functools.partial(kernel, groups, layers), out_shape=jax.S...]
where the time goes in v4:
time: 61.6 us; the launch traced here: 61.4 us
  Pallas kernels  59.9 us (97%)
  local copies, waits for them, and re-layouts  1.47 us (2%)
    pallas_call x1, Pallas kernels, fused(): pl.pallas_call(functools.partial(kernel, groups, layers), out_shape=jax.S...  59.9 us
    unnamed x1, local copies, waits for them, and re-layouts  1.47 us

profile of v4, /device:TPU:0, one launch (start us, length us, event | category | flops | bytes accessed | tf_op | source)
XLA Modules:
  0.0 61.4 jit_solution(13881467338921790858)
XLA Ops:
  0.0 59.9 %shard_map.37 = f32[64,256]{1,0:T(8,128)} custom-call(bf16[2,2,64,1024]{3,2,1,0:T(8,128)(2,1)} %bitcast.1, bf16[1024,1024]{1,0:T(8,128)(2,1)} %p_hbm.1, bf16[256,1024]{1,0:T(8,128)(2,1)} %q_hbm.1), custom_call_target="tpu_custom_call" | custom-call | tf_op jit(solution)/shard_map/pallas_call | solution.py:333
  59.9 1.5 %copy.5 = f32[64,256]{1,0:T(8,128)} copy(f32[64,256]{1,0:T(8,128)} %shard_map.37) | data formatting | bytes 131072
